TPU v7x, 512 devices: a whole 4x4x16 slice. The times are simulated.
512 devices in a mesh: ctx: 128 (over z, x, y_hi), head: 4 (over y_lo, core).
Axes of the slice: x: 4, y: 4 (y_hi: 2, y_lo: 2; y = y_hi * 2 + y_lo), z: 16, core: 2. Of those that a mesh axis runs over, the one named last changes fastest.
Arguments:
- queries: bfloat16 [8192, 8192], P('ctx', 'head'), may hold values from -6 to 6
- keys: bfloat16 [8192, 128], P('ctx'), may hold values from -6 to 6
- key_gain: float32 [128], replicated, may hold values from 0.25 to 1.75
- key_bias: float32 [128], replicated, may hold values from -0.5 to 0.5
- head_weights: bfloat16 [8192, 64], P('ctx', 'head'), may hold values from -6 to 6
- positions: int32 [8192], P('ctx'), may hold values from 0 to 6143, as said below
Outputs:
- index_scores: float32 [8192, 8192], P(('ctx', 'head'))
Inputs may be any that keep to these rules, and one draw needn't show every extreme that they name: `positions`: positions of packed documents: the first 6144 tokens form one document and the rest is split into one to three documents at drawn points; a token's position counts from its document's first token.
All inputs are finite; a program needn't handle non-finite values.
Results may differ from a plain program's by a relative error of at most 0.0095.
Values may be sent and summed in bfloat16 or wider, within the bound.
No kernel may reach another device: no remote copies, remote signals or barrier semaphores. Data moves between devices by JAX's collectives and lax.ppermute only.
A program may use at most 64 MiB of HBM per device.

v0:
```python
import math

import jax
import jax.numpy as jnp
import numpy as np
from jax import lax
from jax.experimental import pallas as pl
from jax.experimental.pallas import tpu as pltpu
from jax.sharding import Mesh
from jax.sharding import PartitionSpec as P

H = 64
DH = 128
ROPE = 64
ROWS = 64
SUB = 16
HG = 16
QT = HG * ROWS
PEERS = 32
SLOTS = 3
NK = PEERS * SUB
PLANE = 512
GROUP = 4 * PLANE
SCALE = 1.0 / math.sqrt(H * DH)


def yarn_frequencies(rope_dims):
    half_dims = rope_dims // 2
    exponent = np.arange(0, rope_dims, 2) / rope_dims
    extra_freq = 1.0 / 10000.0**exponent
    inter_freq = extra_freq / 40.0

    def correction(beta):
        return rope_dims * math.log(4096.0 / (beta * 2.0 * math.pi)) / (2.0 * math.log(10000.0))

    low_dim = max(math.floor(correction(32.0)), 0)
    high_dim = min(math.ceil(correction(1.0)), rope_dims - 1)
    ramp_values = np.clip((np.arange(half_dims) - low_dim) / (high_dim - low_dim), 0.0, 1.0)
    return (inter_freq * ramp_values + extra_freq * (1.0 - ramp_values)).astype(np.float32)


def lane_frequencies():
    f = yarn_frequencies(ROPE)
    return np.concatenate([f, f, np.zeros(DH - ROPE, np.float32)])[None, :]


def turn(x, cosine, sine):
    lane = lax.broadcasted_iota(jnp.int32, x.shape, 1)
    half = ROPE // 2
    other = jnp.where(lane < half, pltpu.roll(x, DH - half, 1), pltpu.roll(x, half, 1))
    return x * cosine + other * sine


def cos_sin(pos, freq):
    angle = pos * freq
    lane = lax.broadcasted_iota(jnp.int32, angle.shape, 1)
    sine = jnp.sin(angle)
    return jnp.cos(angle), jnp.where(lane < ROPE // 2, -sine, sine)


def column(row, n, shift):
    m = row.shape[1]
    at = lax.broadcasted_iota(jnp.int32, (n, m), 0) + shift
    lane = lax.broadcasted_iota(jnp.int32, (n, m), 1)
    return jnp.sum(jnp.where(at == lane, jnp.broadcast_to(row, (n, m)), 0.0), axis=1, keepdims=True)


def where_am_i():
    z_hi, z_lo = lax.axis_index("zh"), lax.axis_index("zl")
    ctx = ((z_hi * 4 + z_lo) * 4 + lax.axis_index("x")) * 2 + lax.axis_index("yh")
    return lax.axis_index("yl") * 2 + lax.axis_index("core"), ctx * ROWS, z_hi


def key_kernel(own, prev, prev2, gain, bias, pos, freq, out):
    head, first, _ = where_am_i()
    off = pl.multiple_of(head * SUB, SUB)
    own_pos = column(pos[...].astype(jnp.float32), SUB, off)
    tok = (lax.broadcasted_iota(jnp.int32, (SUB, 1), 0) + (first + off)).astype(jnp.float32)
    for slot, ref in enumerate((own, prev, prev2)):
        v = ref[pl.ds(off, SUB), :].astype(jnp.float32)
        c = v - jnp.mean(v, axis=-1, keepdims=True)
        s = jnp.mean(c * c, axis=-1, keepdims=True)
        k = c * lax.rsqrt(s + 1e-06) * gain[...] + bias[...]
        p = own_pos if slot == 0 else tok - float(slot * GROUP)
        cosine, sine = cos_sin(p, freq[...])
        r = turn(k, cosine, sine).astype(jnp.bfloat16)
        for d in range(PEERS):
            out[d, slot] = r


def query_kernel(q, w, pos, freq, out):
    angle = freq[...] * pos[...].astype(jnp.float32)
    cosine, sine = jnp.cos(angle), jnp.sin(angle)
    cosine = jnp.concatenate([cosine, cosine], 1)
    sine = jnp.concatenate([sine, sine], 1)
    wf = w[...].astype(jnp.float32)
    both = jnp.concatenate([wf[: HG // 2], wf[HG // 2 :]], 1)
    half = ROPE // 2
    for p in range(HG // 2):
        x = jnp.concatenate(
            [q[:, h * DH : (h + 1) * DH].astype(jnp.float32) for h in (p, p + HG // 2)], 0
        ).T
        a, b = x[:half], x[half:ROPE]
        x = jnp.concatenate([a * cosine - b * sine, b * cosine + a * sine, x[ROPE:]], 0)
        at = slice(p * DH, (p + 1) * DH)
        out[:DH, at] = x.astype(jnp.bfloat16)
        out[DH:, at] = jnp.broadcast_to(both[p : p + 1], (16, DH)).astype(jnp.bfloat16)


def score_kernel(q0, q1, q2, q3, k, pos, out):
    head, first, group = where_am_i()
    row = lax.broadcasted_iota(jnp.int32, (ROWS, 1), 0) + first
    doc = row - column(pos[...].astype(jnp.float32), ROWS, 0).astype(jnp.int32)

    def one(slot):
        kk = k[:, slot].reshape(NK, DH)
        acc = jnp.zeros((NK, DH), jnp.float32)
        for q in (q0, q1, q2, q3):
            w = q[DH : DH + 1, :].astype(jnp.float32)
            for c in range(0, QT, 512):
                s = jnp.dot(kk, q[:DH, c : c + 512], preferred_element_type=jnp.float32)
                for p in range(0, 512, DH):
                    acc = acc + jnp.maximum(s[:, p : p + DH], 0.0) * w[:, c + p : c + p + DH]
        acc = acc.T
        acc = acc[:ROWS] + acc[ROWS:]
        n = lax.broadcasted_iota(jnp.int32, (1, NK), 1)
        key = (group - slot) * GROUP + (n // DH) * PLANE + ((n % DH) // SUB) * ROWS + head * SUB + n % SUB
        seen = (key >= doc) & (key <= row)
        out[:, slot] = jnp.where(seen, acc * SCALE, 0.0).astype(jnp.bfloat16).reshape(4, SUB, NK)

    live = jnp.where(group == 3, 1, group + 1)
    for slot in range(SLOTS):
        @pl.when(slot < live)
        def _():
            one(slot)

        @pl.when(slot >= live)
        def _():
            out[:, slot] = jnp.zeros((4, SUB, NK), jnp.bfloat16)


def place_kernel(parts, out):
    _, _, group = where_am_i()
    out[...] = jnp.zeros_like(out)
    r = lax.broadcasted_iota(jnp.int32, (DH, PLANE), 0)
    c = lax.broadcasted_iota(jnp.int32, (DH, PLANE), 1)
    base = c - ((r // SUB) * ROWS + r % SUB)
    spread = [jnp.where(base == j * SUB, 1.0, 0.0).astype(jnp.bfloat16) for j in range(4)]
    live = jnp.where(group == 3, 1, group + 1)
    for slot in range(SLOTS):
        @pl.when(slot < live)
        def _():
            full = [jnp.zeros((SUB, PLANE), jnp.float32)] * 4
            for j in range(4):
                x = jnp.concatenate([parts[j, slot, :, z * DH : (z + 1) * DH] for z in range(4)], 0)
                y = jnp.dot(x, spread[j], preferred_element_type=jnp.float32)
                full = [full[z] + y[z * SUB : (z + 1) * SUB] for z in range(4)]
            for z in range(4):
                at = pl.multiple_of((group - slot) * GROUP + z * PLANE, PLANE)
                out[:, pl.ds(at, PLANE)] = full[z]


VMEM = pl.BlockSpec(memory_space=pltpu.VMEM)


def call(kernel, shape, dtype, *args, inside=True):
    if inside:
        out = pltpu.VMEM(shape, dtype)
    else:
        out = jax.ShapeDtypeStruct(shape, dtype)
    return pl.pallas_call(kernel, out_shape=out, in_specs=[VMEM] * len(args), out_specs=VMEM)(*args)


def near(x):
    return pltpu.with_memory_space_constraint(x, pltpu.VMEM)


def program(queries, keys, key_gain, key_bias, head_weights, positions):
    freq = lane_frequencies()
    pos = positions.reshape(1, ROWS)

    prev = lax.ppermute(keys, "zh", [(0, 1), (1, 2)])
    relay = lax.ppermute(keys, "zh", [(0, 3)])
    prev2 = lax.ppermute(relay, "zh", [(3, 2)])

    q0 = call(
        query_kernel, (DH + 16, QT), jnp.bfloat16,
        queries, head_weights.T, pos, jnp.asarray(freq[:, : ROPE // 2].T),
    )
    swap = [(0, 1), (1, 0)]
    q1 = lax.ppermute(q0, "yl", swap)
    q2 = lax.ppermute(q0, "core", swap)
    q3 = lax.ppermute(q1, "core", swap)

    sent = call(
        key_kernel, (PEERS, SLOTS, SUB, DH), jnp.bfloat16,
        keys, near(prev), near(prev2), key_gain.reshape(1, DH), key_bias.reshape(1, DH), pos, jnp.asarray(freq),
    )
    k_all = lax.all_to_all(sent, ("zl", "x", "yh"), 0, 0, tiled=True)

    parts = call(
        score_kernel, (4, SLOTS, SUB, NK), jnp.bfloat16,
        near(q0), near(q1), near(q2), near(q3), near(k_all), pos,
    )
    parts = lax.all_to_all(parts, ("yl", "core"), 0, 0, tiled=True)
    return call(place_kernel, (SUB, 8192), jnp.float32, near(parts), inside=False)


def solution(mesh):
    names = ("zh", "zl", "x", "yh", "yl", "core")
    fine = Mesh(mesh.devices.reshape(4, 4, 4, 2, 2, 2), names)
    ctx, head = names[:4], names[4:]
    in_specs = (P(ctx, head), P(ctx, None), P(), P(), P(ctx, head), P(ctx))
    return jax.shard_map(program, mesh=fine, in_specs=in_specs, out_specs=P(names, None), check_vma=False)
```

profile of v0, /device:TPU:368, one launch (start us, length us, event | category | flops | bytes accessed | tf_op | source)
XLA Modules:
  0.0 56.4 jit_solution(529604446246915107)
XLA Ops:
  0.0 0.7 %collective-permute-start.4 = (bf16[64,128]{1,0:T(8,128)(2,1)}, bf16[64,128]{1,0:T(8,128)(2,1)S(1)}, u32[]{:S(2)}, u32[]{:S(2)}) collective-permute-start(bf16[64,128]{1,0:T(8,128)(2,1)} %own.1), channel_id=1, source_target_pairs={{0,384},{1,385},{2,386},{3,387},{4,388},{5,389},{6,390},{7,391},{8... | collective-permute-start | bytes 49160 | tf_op jit(solution)/shard_map/ppermute | solution.py:183
  0.7 1.3 %collective-permute-start.3 = (bf16[64,128]{1,0:T(8,128)(2,1)}, bf16[64,128]{1,0:T(8,128)(2,1)S(1)}, u32[]{:S(2)}, u32[]{:S(2)}) collective-permute-start(bf16[64,128]{1,0:T(8,128)(2,1)} %own.1), channel_id=1, source_target_pairs={{0,128},{128,256},{1,129},{129,257},{2,130},{130,258},{3,131},{131... | collective-permute-start | bytes 49160 | tf_op jit(solution)/shard_map/ppermute | solution.py:182
  2.0 0.0 collective-permute-done.4
  2.0 1.3 %collective-permute-start.5 = (bf16[64,128]{1,0:T(8,128)(2,1)S(1)}, bf16[64,128]{1,0:T(8,128)(2,1)S(1)}, u32[]{:S(2)}, u32[]{:S(2)}) collective-permute-start(bf16[64,128]{1,0:T(8,128)(2,1)S(1)} %collective-permute-done.4), channel_id=1, source_target_pairs={{384,256},{385,257},{386,258},{387,259},{388,260},{389,261},{390,2... | collective-permute-start | bytes 49160 | tf_op jit(solution)/shard_map/ppermute | solution.py:184
  3.3 7.1 %collective-permute-done.3.prev = bf16[64,128]{1,0:T(8,128)(2,1)S(1)} collective-permute-done((bf16[64,128]{1,0:T(8,128)(2,1)}, bf16[64,128]{1,0:T(8,128)(2,1)S(1)}, u32[]{:S(2)}, u32[]{:S(2)}) %collective-permute-start.3) | collective-permute-done | bytes 16416 | tf_op jit(solution)/shard_map/ppermute | solution.py:182
  10.4 4.7 %collective-permute-done.5.prev2 = bf16[64,128]{1,0:T(8,128)(2,1)S(1)} collective-permute-done((bf16[64,128]{1,0:T(8,128)(2,1)S(1)}, bf16[64,128]{1,0:T(8,128)(2,1)S(1)}, u32[]{:S(2)}, u32[]{:S(2)}) %collective-permute-start.5) | collective-permute-done | bytes 16416 | tf_op jit(solution)/shard_map/ppermute | solution.py:184
  15.1 1.8 %shard_map.83 = bf16[32,3,16,128]{3,2,1,0:T(8,128)(2,1)} custom-call(bf16[64,128]{1,0:T(8,128)(2,1)} %own.1, bf16[64,128]{1,0:T(8,128)(2,1)S(1)} %collective-permute-done.3.prev, bf16[64,128]{1,0:T(8,128)(2,1)S(1)} %collective-permute-done.5.prev2, f32[1,128]{1,0:T(1,128)} %bitcast.8, f32[1,128]{1,0:T(1,128)} %bitcast.9, s32[1,64]{1,0:T(1,128)} %bitcast.4, ...), custom_call_target="tpu_custom_call" | custom-call | tf_op jit(solution)/shard_map/pallas_call | solution.py:171
  16.9 10.2 %all-to-all-start = ((bf16[32,3,16,128]{3,2,1,0:T(8,128)(2,1)}), bf16[32,3,16,128]{3,2,1,0:T(8,128)(2,1)S(1)}, u32[]{:S(2)}, u32[]{:S(2)}) async-start(bf16[32,3,16,128]{3,2,1,0:T(8,128)(2,1)} %shard_map.83), calls=%async_computation | async-start | bytes 786432 | tf_op jit(solution)/shard_map/all_to_all | solution.py:199
  27.1 1.2 %shard_map.82.q0 = bf16[144,1024]{1,0:T(8,128)(2,1)S(1)} custom-call(bf16[64,2048]{1,0:T(8,128)(2,1)} %q.1, bf16[16,64]{1,0:T(8,128)(2,1)} %bitcast.7, s32[1,64]{1,0:T(1,128)} %bitcast.5, f32[32,1]{1,0:T(8,128)} %constant.4.clone.freq), custom_call_target="tpu_custom_call" | custom-call | tf_op jit(solution)/shard_map/pallas_call | solution.py:171
  28.3 3.2 %collective-permute-start = (bf16[144,1024]{1,0:T(8,128)(2,1)S(1)}, bf16[144,1024]{1,0:T(8,128)(2,1)S(1)}, u32[]{:S(2)}, u32[]{:S(2)}) collective-permute-start(bf16[144,1024]{1,0:T(8,128)(2,1)S(1)} %shard_map.82.q0), channel_id=1, source_target_pairs={{0,2},{2,0},{1,3},{3,1},{4,6},{6,4},{5,7},{7,5},{8,10},{10,8},{9,1... | collective-permute-start | bytes 884744 | tf_op jit(solution)/shard_map/ppermute | solution.py:191
  31.5 1.9 %collective-permute-start.1 = (bf16[144,1024]{1,0:T(8,128)(2,1)S(1)}, bf16[144,1024]{1,0:T(8,128)(2,1)S(1)}, u32[]{:S(2)}, u32[]{:S(2)}) collective-permute-start(bf16[144,1024]{1,0:T(8,128)(2,1)S(1)} %shard_map.82.q0), channel_id=1, source_target_pairs={{0,1},{1,0},{2,3},{3,2},{4,5},{5,4},{6,7},{7,6},{8,9},{9,8},{10,11... | collective-permute-start | bytes 884744 | tf_op jit(solution)/shard_map/ppermute | solution.py:192
  33.4 5.6 %collective-permute-done.q1 = bf16[144,1024]{1,0:T(8,128)(2,1)S(1)} collective-permute-done((bf16[144,1024]{1,0:T(8,128)(2,1)S(1)}, bf16[144,1024]{1,0:T(8,128)(2,1)S(1)}, u32[]{:S(2)}, u32[]{:S(2)}) %collective-permute-start) | collective-permute-done | bytes 294944 | tf_op jit(solution)/shard_map/ppermute | solution.py:191
  39.0 1.9 %collective-permute-start.2 = (bf16[144,1024]{1,0:T(8,128)(2,1)S(1)}, bf16[144,1024]{1,0:T(8,128)(2,1)S(1)}, u32[]{:S(2)}, u32[]{:S(2)}) collective-permute-start(bf16[144,1024]{1,0:T(8,128)(2,1)S(1)} %collective-permute-done.q1), channel_id=1, source_target_pairs={{0,1},{1,0},{2,3},{3,2},{4,5},{5,4},{6,7},{7,6},{8,9},{9,8},{10,11... | collective-permute-start | bytes 884744 | tf_op jit(solution)/shard_map/ppermute | solution.py:193
  40.9 0.0 collective-permute-done.1.q2
  40.9 1.5 %collective-permute-done.2.q3 = bf16[144,1024]{1,0:T(8,128)(2,1)S(1)} collective-permute-done((bf16[144,1024]{1,0:T(8,128)(2,1)S(1)}, bf16[144,1024]{1,0:T(8,128)(2,1)S(1)}, u32[]{:S(2)}, u32[]{:S(2)}) %collective-permute-start.2) | collective-permute-done | bytes 294944 | tf_op jit(solution)/shard_map/ppermute | solution.py:193
  42.5 0.0 all-to-all-done.k
  42.5 4.7 %shard_map.84 = bf16[4,3,16,512]{3,2,1,0:T(8,128)(2,1)S(1)} custom-call(bf16[144,1024]{1,0:T(8,128)(2,1)S(1)} %shard_map.82.q0, bf16[144,1024]{1,0:T(8,128)(2,1)S(1)} %collective-permute-done.q1, bf16[144,1024]{1,0:T(8,128)(2,1)S(1)} %collective-permute-done.1.q2, bf16[144,1024]{1,0:T(8,128)(2,1)S(1)} %collective-permute-done.2.q3, ...), custom_call_target="tpu_custom_call" | custom-call | tf_op jit(solution)/shard_map/pallas_call | solution.py:171
  47.2 7.7 %all_to_all.10.parts = bf16[4,3,16,512]{3,2,1,0:T(8,128)(2,1)S(1)} all-to-all(bf16[4,3,16,512]{3,2,1,0:T(8,128)(2,1)S(1)} %shard_map.84), channel_id=1, replica_groups=mesh['zh'=4,'zl'=4,'x'=4,'yh'=2,'yl'=2,'core'=2] {'yl','core'}, dimensions={0} | all-to-all | bytes 393216 | tf_op jit(solution)/shard_map/all_to_all | solution.py:205
  54.9 1.5 %shard_map.85 = f32[16,8192]{1,0:T(8,128)} custom-call(bf16[4,3,16,512]{3,2,1,0:T(8,128)(2,1)S(1)} %all_to_all.10.parts), custom_call_target="tpu_custom_call" | custom-call | tf_op jit(solution)/shard_map/pallas_call | solution.py:171
Async XLA Ops:
  0.0 2.0 %collective-permute-start.4 = (bf16[64,128]{1,0:T(8,128)(2,1)}, bf16[64,128]{1,0:T(8,128)(2,1)S(1)}, u32[]{:S(2)}, u32[]{:S(2)}) collective-permute-start(bf16[64,128]{1,0:T(8,128)(2,1)} %own.1), channel_id=1, source_target_pairs={{0,384},{1,385},{2,386},{3,387},{4,388},{5,389},{6,390},{7,391},{8... | collective-permute-start | bytes 49160 | tf_op jit(solution)/shard_map/ppermute | solution.py:183
  0.7 9.8 %collective-permute-start.3 = (bf16[64,128]{1,0:T(8,128)(2,1)}, bf16[64,128]{1,0:T(8,128)(2,1)S(1)}, u32[]{:S(2)}, u32[]{:S(2)}) collective-permute-start(bf16[64,128]{1,0:T(8,128)(2,1)} %own.1), channel_id=1, source_target_pairs={{0,128},{128,256},{1,129},{129,257},{2,130},{130,258},{3,131},{131... | collective-permute-start | bytes 49160 | tf_op jit(solution)/shard_map/ppermute | solution.py:182
  2.0 13.1 %collective-permute-start.5 = (bf16[64,128]{1,0:T(8,128)(2,1)S(1)}, bf16[64,128]{1,0:T(8,128)(2,1)S(1)}, u32[]{:S(2)}, u32[]{:S(2)}) collective-permute-start(bf16[64,128]{1,0:T(8,128)(2,1)S(1)} %collective-permute-done.4), channel_id=1, source_target_pairs={{384,256},{385,257},{386,258},{387,259},{388,260},{389,261},{390,2... | collective-permute-start | bytes 49160 | tf_op jit(solution)/shard_map/ppermute | solution.py:184
  16.9 25.6 %all-to-all-start = ((bf16[32,3,16,128]{3,2,1,0:T(8,128)(2,1)}), bf16[32,3,16,128]{3,2,1,0:T(8,128)(2,1)S(1)}, u32[]{:S(2)}, u32[]{:S(2)}) async-start(bf16[32,3,16,128]{3,2,1,0:T(8,128)(2,1)} %shard_map.83), calls=%async_computation | async-start | bytes 786432 | tf_op jit(solution)/shard_map/all_to_all | solution.py:199
  28.3 10.7 %collective-permute-start = (bf16[144,1024]{1,0:T(8,128)(2,1)S(1)}, bf16[144,1024]{1,0:T(8,128)(2,1)S(1)}, u32[]{:S(2)}, u32[]{:S(2)}) collective-permute-start(bf16[144,1024]{1,0:T(8,128)(2,1)S(1)} %shard_map.82.q0), channel_id=1, source_target_pairs={{0,2},{2,0},{1,3},{3,1},{4,6},{6,4},{5,7},{7,5},{8,10},{10,8},{9,1... | collective-permute-start | bytes 884744 | tf_op jit(solution)/shard_map/ppermute | solution.py:191
  31.5 9.4 %collective-permute-start.1 = (bf16[144,1024]{1,0:T(8,128)(2,1)S(1)}, bf16[144,1024]{1,0:T(8,128)(2,1)S(1)}, u32[]{:S(2)}, u32[]{:S(2)}) collective-permute-start(bf16[144,1024]{1,0:T(8,128)(2,1)S(1)} %shard_map.82.q0), channel_id=1, source_target_pairs={{0,1},{1,0},{2,3},{3,2},{4,5},{5,4},{6,7},{7,6},{8,9},{9,8},{10,11... | collective-permute-start | bytes 884744 | tf_op jit(solution)/shard_map/ppermute | solution.py:192
  39.0 3.5 %collective-permute-start.2 = (bf16[144,1024]{1,0:T(8,128)(2,1)S(1)}, bf16[144,1024]{1,0:T(8,128)(2,1)S(1)}, u32[]{:S(2)}, u32[]{:S(2)}) collective-permute-start(bf16[144,1024]{1,0:T(8,128)(2,1)S(1)} %collective-permute-done.q1), channel_id=1, source_target_pairs={{0,1},{1,0},{2,3},{3,2},{4,5},{5,4},{6,7},{7,6},{8,9},{9,8},{10,11... | collective-permute-start | bytes 884744 | tf_op jit(solution)/shard_map/ppermute | solution.py:193
where the time goes:
time: 56.8 us; the launch traced here: 56.4 us
  starting transfers between devices  20.4 us (36%)
  waiting for transfers between devices  18.9 us (33%)
  Pallas kernels  9.23 us (16%)
  blocking collectives  7.67 us (14%)
    all_to_all x1, starting transfers between devices, program(): k_all = lax.all_to_all(sent, ('zl', 'x', 'yh'), 0, 0, tiled=True)  10.2 us
    pallas_call x4, Pallas kernels, call(): pl.pallas_call(kernel, out_shape=out, in_specs=[VMEM] * len(args), out_sp...  9.23 us
    all_to_all x1, blocking collectives, program(): parts = lax.all_to_all(parts, ('yl', 'core'), 0, 0, tiled=True)  7.67 us
    ppermute x1, waiting for transfers between devices, program(): prev = lax.ppermute(keys, 'zh', [(0, 1), (1, 2)])  7.14 us
    ppermute x1, waiting for transfers between devices, program(): q1 = lax.ppermute(q0, 'yl', swap)  5.57 us
    ppermute x1, waiting for transfers between devices, program(): prev2 = lax.ppermute(relay, 'zh', [(3, 2)])  4.69 us
    ppermute x1, starting transfers between devices, program(): q1 = lax.ppermute(q0, 'yl', swap)  3.19 us
    ppermute x1, starting transfers between devices, program(): q2 = lax.ppermute(q0, 'core', swap)  1.92 us
  transfers between devices with their start and end apart: 7, of which 4 were waited for; matrix products, arithmetic and copies ran while one was open for 0% of the time, Pallas kernels for 2%

commit v1 on v0

--- a/solution.py
+++ b/solution.py
@@ -16,9 +16,9 @@
 SUB = 16
 HG = 16
 QT = HG * ROWS
-PEERS = 32
+PEERS = 8
 SLOTS = 3
-NK = PEERS * SUB
+NK = PEERS * ROWS
 PLANE = 512
 GROUP = 4 * PLANE
 SCALE = 1.0 / math.sqrt(H * DH)
@@ -68,24 +68,27 @@
 def where_am_i():
     z_hi, z_lo = lax.axis_index("zh"), lax.axis_index("zl")
     ctx = ((z_hi * 4 + z_lo) * 4 + lax.axis_index("x")) * 2 + lax.axis_index("yh")
-    return lax.axis_index("yl") * 2 + lax.axis_index("core"), ctx * ROWS, z_hi
-
-
-def key_kernel(own, prev, prev2, gain, bias, pos, freq, out):
-    head, first, _ = where_am_i()
-    off = pl.multiple_of(head * SUB, SUB)
-    own_pos = column(pos[...].astype(jnp.float32), SUB, off)
-    tok = (lax.broadcasted_iota(jnp.int32, (SUB, 1), 0) + (first + off)).astype(jnp.float32)
-    for slot, ref in enumerate((own, prev, prev2)):
-        v = ref[pl.ds(off, SUB), :].astype(jnp.float32)
-        c = v - jnp.mean(v, axis=-1, keepdims=True)
-        s = jnp.mean(c * c, axis=-1, keepdims=True)
-        k = c * lax.rsqrt(s + 1e-06) * gain[...] + bias[...]
-        p = own_pos if slot == 0 else tok - float(slot * GROUP)
-        cosine, sine = cos_sin(p, freq[...])
-        r = turn(k, cosine, sine).astype(jnp.bfloat16)
+    head = lax.axis_index("yl") * 2 + lax.axis_index("core")
+    return head, ctx * ROWS, z_hi, z_lo ^ head ^ (2 * lax.axis_index("yh"))
+
+
+def prepare_kernel(keys, gain, bias, q, w, pos, freq, freq_col, out_k, out_q):
+    v = keys[...].astype(jnp.float32)
+    c = v - jnp.mean(v, axis=-1, keepdims=True)
+    s = jnp.mean(c * c, axis=-1, keepdims=True)
+    k = c * lax.rsqrt(s + 1e-06) * gain[...] + bias[...]
+    cosine, sine = cos_sin(column(pos[...].astype(jnp.float32), ROWS, 0), freq[...])
+    out_k[...] = turn(k, cosine, sine).astype(jnp.bfloat16)
+    query_kernel(q, w, pos, freq_col, out_q)
+
+
+def pack_kernel(mine, own, prev_1, prev_2, prev2, out):
+    _, _, group, z = where_am_i()
+    first = jnp.where(z == lax.axis_index("zl"), mine[...], own[...])
+    prev = jnp.where(group == 1, prev_1[...], prev_2[...])
+    for slot, x in enumerate((first, prev, prev2[...])):
         for d in range(PEERS):
-            out[d, slot] = r
+            out[d, slot] = x
 
 
 def query_kernel(q, w, pos, freq, out):
@@ -108,7 +111,7 @@
 
 
 def score_kernel(q0, q1, q2, q3, k, pos, out):
-    head, first, group = where_am_i()
+    _, first, group, z = where_am_i()
     row = lax.broadcasted_iota(jnp.int32, (ROWS, 1), 0) + first
     doc = row - column(pos[...].astype(jnp.float32), ROWS, 0).astype(jnp.int32)
 
@@ -124,7 +127,7 @@
         acc = acc.T
         acc = acc[:ROWS] + acc[ROWS:]
         n = lax.broadcasted_iota(jnp.int32, (1, NK), 1)
-        key = (group - slot) * GROUP + (n // DH) * PLANE + ((n % DH) // SUB) * ROWS + head * SUB + n % SUB
+        key = (group - slot) * GROUP + z * PLANE + n
         seen = (key >= doc) & (key <= row)
         out[:, slot] = jnp.where(seen, acc * SCALE, 0.0).astype(jnp.bfloat16).reshape(4, SUB, NK)
 
@@ -140,24 +143,15 @@
 
 
 def place_kernel(parts, out):
-    _, _, group = where_am_i()
+    head, _, group, z = where_am_i()
     out[...] = jnp.zeros_like(out)
-    r = lax.broadcasted_iota(jnp.int32, (DH, PLANE), 0)
-    c = lax.broadcasted_iota(jnp.int32, (DH, PLANE), 1)
-    base = c - ((r // SUB) * ROWS + r % SUB)
-    spread = [jnp.where(base == j * SUB, 1.0, 0.0).astype(jnp.bfloat16) for j in range(4)]
     live = jnp.where(group == 3, 1, group + 1)
     for slot in range(SLOTS):
         @pl.when(slot < live)
         def _():
-            full = [jnp.zeros((SUB, PLANE), jnp.float32)] * 4
             for j in range(4):
-                x = jnp.concatenate([parts[j, slot, :, z * DH : (z + 1) * DH] for z in range(4)], 0)
-                y = jnp.dot(x, spread[j], preferred_element_type=jnp.float32)
-                full = [full[z] + y[z * SUB : (z + 1) * SUB] for z in range(4)]
-            for z in range(4):
-                at = pl.multiple_of((group - slot) * GROUP + z * PLANE, PLANE)
-                out[:, pl.ds(at, PLANE)] = full[z]
+                at = pl.multiple_of((group - slot) * GROUP + (z ^ head ^ j) * PLANE, PLANE)
+                out[:, pl.ds(at, PLANE)] = parts[j, slot].astype(jnp.float32)
 
 
 VMEM = pl.BlockSpec(memory_space=pltpu.VMEM)
@@ -175,32 +169,55 @@
     return pltpu.with_memory_space_constraint(x, pltpu.VMEM)
 
 
+LINE = ("zh", "zl", "yh", "yl", "core")
+
+
+def hop(src, dst, cross):
+    def at(g, z, j):
+        return (g * 4 + z) * 8 + j
+
+    return [
+        (at(src, z, j), at(dst, z ^ m if cross else z, j))
+        for z in range(4) for j in range(8) for m in ((j & 3) ^ (j >> 2) * 2,) if src != dst or m
+    ]
+
+
+NEAR = [[(x * 2 + h) * 2 + (t ^ h) for x in range(4) for h in range(2)] for t in range(2)]
+
+
 def program(queries, keys, key_gain, key_bias, head_weights, positions):
     freq = lane_frequencies()
     pos = positions.reshape(1, ROWS)
 
-    prev = lax.ppermute(keys, "zh", [(0, 1), (1, 2)])
-    relay = lax.ppermute(keys, "zh", [(0, 3)])
-    prev2 = lax.ppermute(relay, "zh", [(3, 2)])
-
-    q0 = call(
-        query_kernel, (DH + 16, QT), jnp.bfloat16,
-        queries, head_weights.T, pos, jnp.asarray(freq[:, : ROPE // 2].T),
-    )
+    mine, q0 = pl.pallas_call(
+        prepare_kernel,
+        out_shape=(pltpu.VMEM((ROWS, DH), jnp.bfloat16), pltpu.VMEM((DH + 16, QT), jnp.bfloat16)),
+        in_specs=[VMEM] * 8, out_specs=(VMEM, VMEM), name="prepare",
+    )(
+        keys, key_gain.reshape(1, DH), key_bias.reshape(1, DH), queries, head_weights.T, pos,
+        jnp.asarray(freq), jnp.asarray(freq[:, : ROPE // 2].T),
+    )
+    prev_1 = lax.ppermute(mine, LINE, hop(0, 1, True))
+    prev_2 = lax.ppermute(mine, LINE, hop(1, 2, True))
+    own = lax.ppermute(mine, LINE, sum((hop(g, g, True) for g in range(4)), []))
+    prev2 = lax.ppermute(prev_1, LINE, hop(1, 2, False))
+
     swap = [(0, 1), (1, 0)]
     q1 = lax.ppermute(q0, "yl", swap)
     q2 = lax.ppermute(q0, "core", swap)
     q3 = lax.ppermute(q1, "core", swap)
 
     sent = call(
-        key_kernel, (PEERS, SLOTS, SUB, DH), jnp.bfloat16,
-        keys, near(prev), near(prev2), key_gain.reshape(1, DH), key_bias.reshape(1, DH), pos, jnp.asarray(freq),
-    )
-    k_all = lax.all_to_all(sent, ("zl", "x", "yh"), 0, 0, tiled=True)
+        pack_kernel, (PEERS, SLOTS, ROWS, DH), jnp.bfloat16,
+        near(mine), near(own), near(prev_1), near(prev_2), near(prev2),
+    )
+    k_all = lax.all_to_all(
+        sent, ("x", "yh", "yl"), 0, 0, axis_index_groups=NEAR, tiled=True
+    )
 
     parts = call(
         score_kernel, (4, SLOTS, SUB, NK), jnp.bfloat16,
-        near(q0), near(q1), near(q2), near(q3), near(k_all), pos,
+        near(q0), near(q1), near(q2), near(q3), near(k_all), near(pos),
     )
     parts = lax.all_to_all(parts, ("yl", "core"), 0, 0, tiled=True)
     return call(place_kernel, (SUB, 8192), jnp.float32, near(parts), inside=False)

time: 56.8 us -> 49.3 us (0.87)
  the two profiles are of different devices: /device:TPU:368 before, /device:TPU:1 now
where the time goes in v1:
time: 49.3 us; the launch traced here: 48.9 us
  starting transfers between devices  27.5 us (56%)
  blocking collectives  11.9 us (24%)
  waiting for transfers between devices  4.92 us (10%)
  Pallas kernels  4.48 us (9%)
    all_to_all x1, blocking collectives, program(): parts = lax.all_to_all(parts, ('yl', 'core'), 0, 0, tiled=True)  11.9 us
    ppermute x1, starting transfers between devices, program(): prev_1 = lax.ppermute(mine, LINE, hop(0, 1, True))  10.2 us
    all_to_all x1, starting transfers between devices, program(): lax.all_to_all(sent, ('x', 'yh', 'yl'), 0, 0, axis_index_groups=NEAR, til...  5.77 us
    ppermute x1, starting transfers between devices, program(): q1 = lax.ppermute(q0, 'yl', swap)  4.02 us
    all_to_all x1, waiting for transfers between devices, program(): lax.all_to_all(sent, ('x', 'yh', 'yl'), 0, 0, axis_index_groups=NEAR, til...  3.7 us
    pallas_call x3, Pallas kernels, call(): pl.pallas_call(kernel, out_shape=out, in_specs=[VMEM] * len(args), out_sp...  3.09 us
    ppermute x1, starting transfers between devices, program(): q3 = lax.ppermute(q1, 'core', swap)  2.41 us
    ppermute x1, starting transfers between devices, program(): own = lax.ppermute(mine, LINE, sum((hop(g, g, True) for g in range(4)), []))  1.92 us
  transfers between devices with their start and end apart: 8, of which 2 were waited for; matrix products, arithmetic and copies ran while one was open for 0% of the time, Pallas kernels for 2%

profile of v1, /device:TPU:1, one launch (start us, length us, event | category | flops | bytes accessed | tf_op | source)
XLA Modules:
  0.0 48.9 jit_solution(12698430741395901076)
XLA Ops:
  0.0 1.4 %prepare.1 = (bf16[64,128]{1,0:T(8,128)(2,1)S(1)}, bf16[144,1024]{1,0:T(8,128)(2,1)S(1)}) custom-call(bf16[64,128]{1,0:T(8,128)(2,1)} %keys.1, f32[1,128]{1,0:T(1,128)} %bitcast.7, f32[1,128]{1,0:T(1,128)} %bitcast.8, bf16[64,2048]{1,0:T(8,128)(2,1)} %q.1, bf16[16,64]{1,0:T(8,128)(2,1)} %bitcast.6, s32[1,64]{1,0:T(1,128)} %bitcast.4, ...), custom_call_target="tpu_custom_call" | custom-call | tf_op jit(solution)/shard_map/prepare/pallas_call | solution.py:192
  1.4 4.0 %collective-permute-start = (bf16[144,1024]{1,0:T(8,128)(2,1)S(1)}, bf16[144,1024]{1,0:T(8,128)(2,1)S(1)}, u32[]{:S(2)}, u32[]{:S(2)}) collective-permute-start(bf16[144,1024]{1,0:T(8,128)(2,1)S(1)} %get-tuple-element.7.q0), channel_id=1, source_target_pairs={{0,2},{2,0},{1,3},{3,1},{4,6},{6,4},{5,7},{7,5},{8,10},{10,8},{9,1... | collective-permute-start | bytes 884744 | tf_op jit(solution)/shard_map/ppermute | solution.py:206
  5.4 10.2 %collective-permute-start.4 = (bf16[64,128]{1,0:T(8,128)(2,1)S(1)}, bf16[64,128]{1,0:T(8,128)(2,1)S(1)}, u32[]{:S(2)}, u32[]{:S(2)}) collective-permute-start(bf16[64,128]{1,0:T(8,128)(2,1)S(1)} %get-tuple-element.8.mine), channel_id=1, source_target_pairs={{0,128},{1,161},{2,194},{3,227},{4,196},{5,229},{6,134},{7,167},{3... | collective-permute-start | bytes 49160 | tf_op jit(solution)/shard_map/ppermute | solution.py:200
  15.6 1.9 %collective-permute-start.3 = (bf16[64,128]{1,0:T(8,128)(2,1)S(1)}, bf16[64,128]{1,0:T(8,128)(2,1)S(1)}, u32[]{:S(2)}, u32[]{:S(2)}) collective-permute-start(bf16[64,128]{1,0:T(8,128)(2,1)S(1)} %get-tuple-element.8.mine), channel_id=1, source_target_pairs={{1,33},{2,66},{3,99},{4,68},{5,101},{7,39},{33,1},{34,98},{35,67},... | collective-permute-start | bytes 49160 | tf_op jit(solution)/shard_map/ppermute | solution.py:202
  17.5 0.7 %collective-permute-start.5 = (bf16[64,128]{1,0:T(8,128)(2,1)S(1)}, bf16[64,128]{1,0:T(8,128)(2,1)S(1)}, u32[]{:S(2)}, u32[]{:S(2)}) collective-permute-start(bf16[64,128]{1,0:T(8,128)(2,1)S(1)} %get-tuple-element.8.mine), channel_id=1, source_target_pairs={{128,256},{129,289},{130,322},{131,355},{132,324},{133,357},{134,2... | collective-permute-start | bytes 49160 | tf_op jit(solution)/shard_map/ppermute | solution.py:201
  18.2 0.0 collective-permute-done.4.prev_1
  18.2 0.7 %collective-permute-start.6 = (bf16[64,128]{1,0:T(8,128)(2,1)S(1)}, bf16[64,128]{1,0:T(8,128)(2,1)S(1)}, u32[]{:S(2)}, u32[]{:S(2)}) collective-permute-start(bf16[64,128]{1,0:T(8,128)(2,1)S(1)} %collective-permute-done.4.prev_1), channel_id=1, source_target_pairs={{128,256},{129,257},{130,258},{131,259},{132,260},{133,261},{134,2... | collective-permute-start | bytes 49160 | tf_op jit(solution)/shard_map/ppermute | solution.py:203
  18.9 1.2 %collective-permute-done.3.own = bf16[64,128]{1,0:T(8,128)(2,1)S(1)} collective-permute-done((bf16[64,128]{1,0:T(8,128)(2,1)S(1)}, bf16[64,128]{1,0:T(8,128)(2,1)S(1)}, u32[]{:S(2)}, u32[]{:S(2)}) %collective-permute-start.3) | collective-permute-done | bytes 16416 | tf_op jit(solution)/shard_map/ppermute | solution.py:202
  20.1 0.0 collective-permute-done.5.prev_2
  20.1 0.0 collective-permute-done.6.prev2
  20.1 0.8 %shard_map.82 = bf16[8,3,64,128]{3,2,1,0:T(8,128)(2,1)} custom-call(bf16[64,128]{1,0:T(8,128)(2,1)S(1)} %get-tuple-element.8.mine, bf16[64,128]{1,0:T(8,128)(2,1)S(1)} %collective-permute-done.3.own, bf16[64,128]{1,0:T(8,128)(2,1)S(1)} %collective-permute-done.4.prev_1, bf16[64,128]{1,0:T(8,128)(2,1)S(1)} %collective-permute-done.5.prev_2, ...), custom_call_target="tpu_custom_call" | custom-call | tf_op jit(solution)/shard_map/pallas_call | solution.py:165
  20.9 0.0 copy-start
  20.9 5.8 %all-to-all-start = ((bf16[8,3,64,128]{3,2,1,0:T(8,128)(2,1)}), bf16[8,3,64,128]{3,2,1,0:T(8,128)(2,1)S(1)}, u32[]{:S(2)}, u32[]{:S(2)}) async-start(bf16[8,3,64,128]{3,2,1,0:T(8,128)(2,1)} %shard_map.82), calls=%async_computation | async-start | bytes 786432 | tf_op jit(solution)/shard_map/all_to_all | solution.py:214
  26.7 1.9 %collective-permute-start.1 = (bf16[144,1024]{1,0:T(8,128)(2,1)S(1)}, bf16[144,1024]{1,0:T(8,128)(2,1)S(1)}, u32[]{:S(2)}, u32[]{:S(2)}) collective-permute-start(bf16[144,1024]{1,0:T(8,128)(2,1)S(1)} %get-tuple-element.7.q0), channel_id=1, source_target_pairs={{0,1},{1,0},{2,3},{3,2},{4,5},{5,4},{6,7},{7,6},{8,9},{9,8},{10,11... | collective-permute-start | bytes 884744 | tf_op jit(solution)/shard_map/ppermute | solution.py:207
  28.6 0.0 collective-permute-done.q1
  28.6 2.4 %collective-permute-start.2 = (bf16[144,1024]{1,0:T(8,128)(2,1)S(1)}, bf16[144,1024]{1,0:T(8,128)(2,1)S(1)}, u32[]{:S(2)}, u32[]{:S(2)}) collective-permute-start(bf16[144,1024]{1,0:T(8,128)(2,1)S(1)} %collective-permute-done.q1), channel_id=1, source_target_pairs={{0,1},{1,0},{2,3},{3,2},{4,5},{5,4},{6,7},{7,6},{8,9},{9,8},{10,11... | collective-permute-start | bytes 884744 | tf_op jit(solution)/shard_map/ppermute | solution.py:208
  31.0 0.0 collective-permute-done.1.q2
  31.0 3.7 %all-to-all-done.k = bf16[8,3,64,128]{3,2,1,0:T(8,128)(2,1)S(1)} async-done(((bf16[8,3,64,128]{3,2,1,0:T(8,128)(2,1)}), bf16[8,3,64,128]{3,2,1,0:T(8,128)(2,1)S(1)}, u32[]{:S(2)}, u32[]{:S(2)}) %all-to-all-start) | async-done | bytes 393248 | tf_op jit(solution)/shard_map/all_to_all | solution.py:214
  34.7 0.0 collective-permute-done.2.q3
  34.7 0.0 copy-done
  34.7 1.4 %shard_map.83 = bf16[4,3,16,512]{3,2,1,0:T(8,128)(2,1)S(1)} custom-call(bf16[144,1024]{1,0:T(8,128)(2,1)S(1)} %get-tuple-element.7.q0, bf16[144,1024]{1,0:T(8,128)(2,1)S(1)} %collective-permute-done.q1, bf16[144,1024]{1,0:T(8,128)(2,1)S(1)} %collective-permute-done.1.q2, bf16[144,1024]{1,0:T(8,128)(2,1)S(1)} %collective-permute-done.2.q3, ...), custom_call_target="tpu_custom_call" | custom-call | tf_op jit(solution)/shard_map/pallas_call | solution.py:165
  36.2 11.9 %all_to_all.10.parts = bf16[4,3,16,512]{3,2,1,0:T(8,128)(2,1)S(1)} all-to-all(bf16[4,3,16,512]{3,2,1,0:T(8,128)(2,1)S(1)} %shard_map.83), channel_id=1, replica_groups=mesh['zh'=4,'zl'=4,'x'=4,'yh'=2,'yl'=2,'core'=2] {'yl','core'}, dimensions={0} | all-to-all | bytes 393216 | tf_op jit(solution)/shard_map/all_to_all | solution.py:222
  48.0 0.8 %shard_map.84 = f32[16,8192]{1,0:T(8,128)} custom-call(bf16[4,3,16,512]{3,2,1,0:T(8,128)(2,1)S(1)} %all_to_all.10.parts), custom_call_target="tpu_custom_call" | custom-call | tf_op jit(solution)/shard_map/pallas_call | solution.py:165
Async XLA Ops:
  1.4 27.2 %collective-permute-start = (bf16[144,1024]{1,0:T(8,128)(2,1)S(1)}, bf16[144,1024]{1,0:T(8,128)(2,1)S(1)}, u32[]{:S(2)}, u32[]{:S(2)}) collective-permute-start(bf16[144,1024]{1,0:T(8,128)(2,1)S(1)} %get-tuple-element.7.q0), channel_id=1, source_target_pairs={{0,2},{2,0},{1,3},{3,1},{4,6},{6,4},{5,7},{7,5},{8,10},{10,8},{9,1... | collective-permute-start | bytes 884744 | tf_op jit(solution)/shard_map/ppermute | solution.py:206
  5.4 12.8 %collective-permute-start.4 = (bf16[64,128]{1,0:T(8,128)(2,1)S(1)}, bf16[64,128]{1,0:T(8,128)(2,1)S(1)}, u32[]{:S(2)}, u32[]{:S(2)}) collective-permute-start(bf16[64,128]{1,0:T(8,128)(2,1)S(1)} %get-tuple-element.8.mine), channel_id=1, source_target_pairs={{0,128},{1,161},{2,194},{3,227},{4,196},{5,229},{6,134},{7,167},{3... | collective-permute-start | bytes 49160 | tf_op jit(solution)/shard_map/ppermute | solution.py:200
  15.6 4.5 %collective-permute-start.3 = (bf16[64,128]{1,0:T(8,128)(2,1)S(1)}, bf16[64,128]{1,0:T(8,128)(2,1)S(1)}, u32[]{:S(2)}, u32[]{:S(2)}) collective-permute-start(bf16[64,128]{1,0:T(8,128)(2,1)S(1)} %get-tuple-element.8.mine), channel_id=1, source_target_pairs={{1,33},{2,66},{3,99},{4,68},{5,101},{7,39},{33,1},{34,98},{35,67},... | collective-permute-start | bytes 49160 | tf_op jit(solution)/shard_map/ppermute | solution.py:202
  17.5 2.6 %collective-permute-start.5 = (bf16[64,128]{1,0:T(8,128)(2,1)S(1)}, bf16[64,128]{1,0:T(8,128)(2,1)S(1)}, u32[]{:S(2)}, u32[]{:S(2)}) collective-permute-start(bf16[64,128]{1,0:T(8,128)(2,1)S(1)} %get-tuple-element.8.mine), channel_id=1, source_target_pairs={{128,256},{129,289},{130,322},{131,355},{132,324},{133,357},{134,2... | collective-permute-start | bytes 49160 | tf_op jit(solution)/shard_map/ppermute | solution.py:201
  18.2 1.9 %collective-permute-start.6 = (bf16[64,128]{1,0:T(8,128)(2,1)S(1)}, bf16[64,128]{1,0:T(8,128)(2,1)S(1)}, u32[]{:S(2)}, u32[]{:S(2)}) collective-permute-start(bf16[64,128]{1,0:T(8,128)(2,1)S(1)} %collective-permute-done.4.prev_1), channel_id=1, source_target_pairs={{128,256},{129,257},{130,258},{131,259},{132,260},{133,261},{134,2... | collective-permute-start | bytes 49160 | tf_op jit(solution)/shard_map/ppermute | solution.py:203
  20.9 13.8 %copy-start = (s32[64]{0:T(128)S(1)}, s32[64]{0:T(128)}, u32[]{:S(2)}) copy-start(s32[64]{0:T(128)} %param.13) | copy-start | bytes 772
  20.9 13.8 %all-to-all-start = ((bf16[8,3,64,128]{3,2,1,0:T(8,128)(2,1)}), bf16[8,3,64,128]{3,2,1,0:T(8,128)(2,1)S(1)}, u32[]{:S(2)}, u32[]{:S(2)}) async-start(bf16[8,3,64,128]{3,2,1,0:T(8,128)(2,1)} %shard_map.82), calls=%async_computation | async-start | bytes 786432 | tf_op jit(solution)/shard_map/all_to_all | solution.py:214
  26.7 4.3 %collective-permute-start.1 = (bf16[144,1024]{1,0:T(8,128)(2,1)S(1)}, bf16[144,1024]{1,0:T(8,128)(2,1)S(1)}, u32[]{:S(2)}, u32[]{:S(2)}) collective-permute-start(bf16[144,1024]{1,0:T(8,128)(2,1)S(1)} %get-tuple-element.7.q0), channel_id=1, source_target_pairs={{0,1},{1,0},{2,3},{3,2},{4,5},{5,4},{6,7},{7,6},{8,9},{9,8},{10,11... | collective-permute-start | bytes 884744 | tf_op jit(solution)/shard_map/ppermute | solution.py:207
  28.6 6.1 %collective-permute-start.2 = (bf16[144,1024]{1,0:T(8,128)(2,1)S(1)}, bf16[144,1024]{1,0:T(8,128)(2,1)S(1)}, u32[]{:S(2)}, u32[]{:S(2)}) collective-permute-start(bf16[144,1024]{1,0:T(8,128)(2,1)S(1)} %collective-permute-done.q1), channel_id=1, source_target_pairs={{0,1},{1,0},{2,3},{3,2},{4,5},{5,4},{6,7},{7,6},{8,9},{9,8},{10,11... | collective-permute-start | bytes 884744 | tf_op jit(solution)/shard_map/ppermute | solution.py:208

commit v2 on v1

--- a/solution.py
+++ b/solution.py
@@ -21,6 +21,7 @@
 NK = PEERS * ROWS
 PLANE = 512
 GROUP = 4 * PLANE
+LAST_EARLY = 6
 SCALE = 1.0 / math.sqrt(H * DH)
 
 
@@ -39,23 +40,20 @@
     return (inter_freq * ramp_values + extra_freq * (1.0 - ramp_values)).astype(np.float32)
 
 
-def lane_frequencies():
-    f = yarn_frequencies(ROPE)
-    return np.concatenate([f, f, np.zeros(DH - ROPE, np.float32)])[None, :]
-
-
-def turn(x, cosine, sine):
-    lane = lax.broadcasted_iota(jnp.int32, x.shape, 1)
+def turned(raw, gain, bias, cosine, sine):
+    v = raw.astype(jnp.float32)
+    c = v - jnp.mean(v, axis=-1, keepdims=True)
+    s = jnp.mean(c * c, axis=-1, keepdims=True)
+    k = c * lax.rsqrt(s + 1e-06) * gain + bias
+    return rotated(jnp.concatenate([k, k], 0).T, cosine, sine).T[:ROWS].astype(jnp.bfloat16)
+
+
+def rotated(x, cosine, sine):
     half = ROPE // 2
-    other = jnp.where(lane < half, pltpu.roll(x, DH - half, 1), pltpu.roll(x, half, 1))
-    return x * cosine + other * sine
-
-
-def cos_sin(pos, freq):
-    angle = pos * freq
-    lane = lax.broadcasted_iota(jnp.int32, angle.shape, 1)
-    sine = jnp.sin(angle)
-    return jnp.cos(angle), jnp.where(lane < ROPE // 2, -sine, sine)
+    cosine = jnp.concatenate([cosine, cosine], 1)
+    sine = jnp.concatenate([sine, sine], 1)
+    a, b = x[:half], x[half:ROPE]
+    return jnp.concatenate([a * cosine - b * sine, b * cosine + a * sine, x[ROPE:]], 0)
 
 
 def column(row, n, shift):
@@ -72,14 +70,92 @@
     return head, ctx * ROWS, z_hi, z_lo ^ head ^ (2 * lax.axis_index("yh"))
 
 
-def prepare_kernel(keys, gain, bias, q, w, pos, freq, freq_col, out_k, out_q):
-    v = keys[...].astype(jnp.float32)
-    c = v - jnp.mean(v, axis=-1, keepdims=True)
-    s = jnp.mean(c * c, axis=-1, keepdims=True)
-    k = c * lax.rsqrt(s + 1e-06) * gain[...] + bias[...]
-    cosine, sine = cos_sin(column(pos[...].astype(jnp.float32), ROWS, 0), freq[...])
-    out_k[...] = turn(k, cosine, sine).astype(jnp.bfloat16)
-    query_kernel(q, w, pos, freq_col, out_q)
+def turn_queries(q, w, cosine, sine, out):
+    wf = w[...].astype(jnp.float32)
+    both = jnp.concatenate([wf[: HG // 2], wf[HG // 2 :]], 1)
+    for p in range(HG // 2):
+        x = jnp.concatenate(
+            [q[:, h * DH : (h + 1) * DH].astype(jnp.float32) for h in (p, p + HG // 2)], 0
+        ).T
+        at = slice(p * DH, (p + 1) * DH)
+        out[:DH, at] = rotated(x, cosine, sine).astype(jnp.bfloat16)
+        out[DH:, at] = jnp.broadcast_to(both[p : p + 1], (16, DH)).astype(jnp.bfloat16)
+
+
+def is_early():
+    return lax.axis_index("zh") * 4 + lax.axis_index("zl") <= LAST_EARLY
+
+
+def sends_on():
+    return lax.axis_index("zh") < 2
+
+
+def fetch(pairs, sems):
+    copies = [pltpu.make_async_copy(src, dst, sems.at[i]) for i, (src, dst) in enumerate(pairs)]
+    for c in copies:
+        c.start()
+    for c in copies:
+        c.wait()
+
+
+def early_kernel(*refs):
+    far, out_k, out_q, held, sems = refs[:7], refs[7], refs[8], refs[9:16], refs[16]
+
+    @pl.when(is_early())
+    def _():
+        fetch(zip(far, held), sems)
+        keys, gain, bias, pos, freq, w, q = held
+        angle = freq[...] * pos[...].astype(jnp.float32)
+        cosine, sine = jnp.cos(angle), jnp.sin(angle)
+        out_k[...] = turned(keys[...], gain[...], bias[...], cosine, sine)
+        turn_queries(q, w, cosine, sine, out_q)
+
+
+def late_keys_kernel(*refs):
+    far, before, out_q, out_k, held, sems = refs[:7], refs[8], refs[9], refs[10], refs[11:18], refs[18]
+    keys, gain, bias, pos, freq, w, q = held
+    late = jnp.logical_not(is_early())
+
+    @pl.when(is_early())
+    def _():
+        out_k[...] = before[...]
+
+    @pl.when(late & sends_on())
+    def _():
+        fetch(zip(far, held), sems)
+        angle = freq[...] * pos[...].astype(jnp.float32)
+        cosine, sine = jnp.cos(angle), jnp.sin(angle)
+        out_k[...] = turned(keys[...], gain[...], bias[...], cosine, sine)
+        turn_queries(q, w, cosine, sine, out_q)
+
+    @pl.when(late & jnp.logical_not(sends_on()))
+    def _():
+        fetch(tuple(zip(far, held))[:5], sems)
+        angle = freq[...] * pos[...].astype(jnp.float32)
+        out_k[...] = turned(keys[...], gain[...], bias[...], jnp.cos(angle), jnp.sin(angle))
+
+
+def late_queries_kernel(*refs):
+    far, out_q, held, sems = refs[:4], refs[5], refs[6:10], refs[10]
+
+    @pl.when(jnp.logical_not(is_early() | sends_on()))
+    def _():
+        fetch(zip(far, held), sems)
+        pos, freq, w, q = held
+        angle = freq[...] * pos[...].astype(jnp.float32)
+        turn_queries(q, w, jnp.cos(angle), jnp.sin(angle), out_q)
+
+
+def prepare(kernel, sources, shapes, before=(), kept=0):
+    n = len(sources)
+    return pl.pallas_call(
+        kernel,
+        out_shape=tuple(pltpu.VMEM(shape, jnp.bfloat16) for shape in shapes),
+        in_specs=[ANY] * n + [VMEM] * len(before),
+        out_specs=(VMEM,) * len(shapes),
+        input_output_aliases={n + i: i for i in range(kept)},
+        scratch_shapes=[pltpu.VMEM(x.shape, x.dtype) for x in sources] + [pltpu.SemaphoreType.DMA((n,))],
+    )(*sources, *[near(x) for x in before])
 
 
 def pack_kernel(mine, own, prev_1, prev_2, prev2, out):
@@ -91,33 +167,15 @@
             out[d, slot] = x
 
 
-def query_kernel(q, w, pos, freq, out):
-    angle = freq[...] * pos[...].astype(jnp.float32)
-    cosine, sine = jnp.cos(angle), jnp.sin(angle)
-    cosine = jnp.concatenate([cosine, cosine], 1)
-    sine = jnp.concatenate([sine, sine], 1)
-    wf = w[...].astype(jnp.float32)
-    both = jnp.concatenate([wf[: HG // 2], wf[HG // 2 :]], 1)
-    half = ROPE // 2
-    for p in range(HG // 2):
-        x = jnp.concatenate(
-            [q[:, h * DH : (h + 1) * DH].astype(jnp.float32) for h in (p, p + HG // 2)], 0
-        ).T
-        a, b = x[:half], x[half:ROPE]
-        x = jnp.concatenate([a * cosine - b * sine, b * cosine + a * sine, x[ROPE:]], 0)
-        at = slice(p * DH, (p + 1) * DH)
-        out[:DH, at] = x.astype(jnp.bfloat16)
-        out[DH:, at] = jnp.broadcast_to(both[p : p + 1], (16, DH)).astype(jnp.bfloat16)
-
-
 def score_kernel(q0, q1, q2, q3, k, pos, out):
     _, first, group, z = where_am_i()
     row = lax.broadcasted_iota(jnp.int32, (ROWS, 1), 0) + first
     doc = row - column(pos[...].astype(jnp.float32), ROWS, 0).astype(jnp.int32)
 
-    def one(slot):
-        kk = k[:, slot].reshape(NK, DH)
-        acc = jnp.zeros((NK, DH), jnp.float32)
+    def one(slot, start, n):
+        peers = slice(start // ROWS, (start + n) // ROWS)
+        kk = k[peers, slot].reshape(n, DH)
+        acc = jnp.zeros((n, DH), jnp.float32)
         for q in (q0, q1, q2, q3):
             w = q[DH : DH + 1, :].astype(jnp.float32)
             for c in range(0, QT, 512):
@@ -126,18 +184,34 @@
                     acc = acc + jnp.maximum(s[:, p : p + DH], 0.0) * w[:, c + p : c + p + DH]
         acc = acc.T
         acc = acc[:ROWS] + acc[ROWS:]
-        n = lax.broadcasted_iota(jnp.int32, (1, NK), 1)
-        key = (group - slot) * GROUP + z * PLANE + n
+        key = plane_start(slot) + start + lax.broadcasted_iota(jnp.int32, (1, n), 1)
         seen = (key >= doc) & (key <= row)
-        out[:, slot] = jnp.where(seen, acc * SCALE, 0.0).astype(jnp.bfloat16).reshape(4, SUB, NK)
-
-    live = jnp.where(group == 3, 1, group + 1)
-    for slot in range(SLOTS):
-        @pl.when(slot < live)
-        def _():
-            one(slot)
-
-        @pl.when(slot >= live)
+        out[:, slot, :, start : start + n] = (
+            jnp.where(seen, acc * SCALE, 0.0).astype(jnp.bfloat16).reshape(4, SUB, n)
+        )
+
+    def plane_start(slot):
+        return (group - slot) * GROUP + z * PLANE
+
+    for start, n in ((0, 128), (128, 128), (256, 256)):
+        reached = plane_start(0) + start < first + ROWS
+
+        @pl.when(reached)
+        def _():
+            one(0, start, n)
+
+        @pl.when(jnp.logical_not(reached))
+        def _():
+            out[:, 0, :, start : start + n] = jnp.zeros((4, SUB, n), jnp.bfloat16)
+
+    for slot in range(1, SLOTS):
+        live = (slot <= group) & (group < 3)
+
+        @pl.when(live)
+        def _():
+            one(slot, 0, NK)
+
+        @pl.when(jnp.logical_not(live))
         def _():
             out[:, slot] = jnp.zeros((4, SUB, NK), jnp.bfloat16)
 
@@ -155,6 +229,7 @@
 
 
 VMEM = pl.BlockSpec(memory_space=pltpu.VMEM)
+ANY = pl.BlockSpec(memory_space=pl.ANY)
 
 
 def call(kernel, shape, dtype, *args, inside=True):
@@ -186,22 +261,23 @@
 
 
 def program(queries, keys, key_gain, key_bias, head_weights, positions):
-    freq = lane_frequencies()
+    freq = jnp.asarray(yarn_frequencies(ROPE)[:, None])
+    gain, bias = key_gain.reshape(1, DH), key_bias.reshape(1, DH)
     pos = positions.reshape(1, ROWS)
-
-    mine, q0 = pl.pallas_call(
-        prepare_kernel,
-        out_shape=(pltpu.VMEM((ROWS, DH), jnp.bfloat16), pltpu.VMEM((DH + 16, QT), jnp.bfloat16)),
-        in_specs=[VMEM] * 8, out_specs=(VMEM, VMEM), name="prepare",
-    )(
-        keys, key_gain.reshape(1, DH), key_bias.reshape(1, DH), queries, head_weights.T, pos,
-        jnp.asarray(freq), jnp.asarray(freq[:, : ROPE // 2].T),
+    weights = head_weights.T
+
+    key_shape, query_shape = (ROWS, DH), (DH + 16, QT)
+
+    mine, q_early = prepare(early_kernel, (keys, gain, bias, pos, freq, weights, queries), (key_shape, query_shape))
+    prev_1 = lax.ppermute(mine, LINE, hop(0, 1, True))
+    q_early, mine = prepare(
+        late_keys_kernel, (keys, gain, bias, pos, freq, weights, queries),
+        (query_shape, key_shape), (q_early, mine), 1,
     )
-    prev_1 = lax.ppermute(mine, LINE, hop(0, 1, True))
     prev_2 = lax.ppermute(mine, LINE, hop(1, 2, True))
     own = lax.ppermute(mine, LINE, sum((hop(g, g, True) for g in range(4)), []))
     prev2 = lax.ppermute(prev_1, LINE, hop(1, 2, False))
-
+    (q0,) = prepare(late_queries_kernel, (pos, freq, weights, queries), (query_shape,), (q_early,), 1)
     swap = [(0, 1), (1, 0)]
     q1 = lax.ppermute(q0, "yl", swap)
     q2 = lax.ppermute(q0, "core", swap)

time: 49.3 us -> 49.4 us (level)
  the two profiles are of different devices: /device:TPU:1 before, /device:TPU:352 now
where the time goes in v2:
time: 49.4 us; the launch traced here: 48.9 us
  starting transfers between devices  17.8 us (36%)
  waiting for transfers between devices  14.5 us (29%)
  blocking collectives  8.98 us (18%)
  Pallas kernels  7.54 us (15%)
    all_to_all x1, blocking collectives, program(): parts = lax.all_to_all(parts, ('yl', 'core'), 0, 0, tiled=True)  8.98 us
    ppermute x1, waiting for transfers between devices, program(): prev_2 = lax.ppermute(mine, LINE, hop(1, 2, True))  6.98 us
    all_to_all x1, starting transfers between devices, program(): lax.all_to_all(sent, ('x', 'yh', 'yl'), 0, 0, axis_index_groups=NEAR, til...  6.05 us
    pallas_call x3, Pallas kernels, call(): pl.pallas_call(kernel, out_shape=out, in_specs=[VMEM] * len(args), out_sp...  4.93 us
    all_to_all x1, waiting for transfers between devices, program(): lax.all_to_all(sent, ('x', 'yh', 'yl'), 0, 0, axis_index_groups=NEAR, til...  4.53 us
    ppermute x1, starting transfers between devices, program(): q1 = lax.ppermute(q0, 'yl', swap)  3.48 us
    ppermute x1, waiting for transfers between devices, program(): prev2 = lax.ppermute(prev_1, LINE, hop(1, 2, False))  2.96 us
    pallas_call x3, Pallas kernels, prepare(): pl.pallas_call(kernel, out_shape=tuple((pltpu.VMEM(shape, jnp.bfloat16) f...  2.61 us
  transfers between devices with their start and end apart: 8, of which 3 were waited for; matrix products, arithmetic and copies ran while one was open for 0% of the time, Pallas kernels for 2%

profile of v2, /device:TPU:352, one launch (start us, length us, event | category | flops | bytes accessed | tf_op | source)
XLA Modules:
  0.0 48.9 jit_solution(1422137575140838780)
XLA Ops:
  0.0 0.1 shard_map.73
  0.1 1.2 %shard_map.74 = (bf16[144,1024]{1,0:T(8,128)(2,1)S(1)}, bf16[64,128]{1,0:T(8,128)(2,1)S(1)}) custom-call(bf16[64,128]{1,0:T(8,128)(2,1)} %refs_0_.3, f32[1,128]{1,0:T(1,128)} %bitcast.12, f32[1,128]{1,0:T(1,128)} %bitcast.14, s32[1,64]{1,0:T(1,128)} %bitcast.5, f32[32,1]{1,0:T(8,128)} %constant.2.clone.refs_4_.refs_1_, ...), custom_call_target="tpu_custom_call", output_to_operand_aliasing={{0}: (7, {})} | custom-call | tf_op jit(solution)/shard_map/pallas_call | solution.py:151
  1.3 1.3 %shard_map.75.q0 = bf16[144,1024]{1,0:T(8,128)(2,1)S(1)} custom-call(s32[1,64]{1,0:T(1,128)} %bitcast.6, f32[32,1]{1,0:T(8,128)} %constant.2.clone.refs_4_.refs_1_, bf16[16,64]{1,0:T(8,128)(2,1)} %bitcast.10, bf16[64,2048]{1,0:T(8,128)(2,1)} %refs_3_.1, bf16[144,1024]{1,0:T(8,128)(2,1)S(1)} %get-tuple-element.11.refs_4_), custom_call_target="tpu_custom_call", output_to_operand_aliasing={{}: (4, {})} | custom-call | tf_op jit(solution)/shard_map/pallas_call | solution.py:151
  2.6 3.5 %collective-permute-start = (bf16[144,1024]{1,0:T(8,128)(2,1)S(1)}, bf16[144,1024]{1,0:T(8,128)(2,1)S(1)}, u32[]{:S(2)}, u32[]{:S(2)}) collective-permute-start(bf16[144,1024]{1,0:T(8,128)(2,1)S(1)} %shard_map.75.q0), channel_id=1, source_target_pairs={{0,2},{2,0},{1,3},{3,1},{4,6},{6,4},{5,7},{7,5},{8,10},{10,8},{9,1... | collective-permute-start | bytes 884744 | tf_op jit(solution)/shard_map/ppermute | solution.py:282
  6.1 0.7 %collective-permute-start.4 = (bf16[64,128]{1,0:T(8,128)(2,1)S(1)}, bf16[64,128]{1,0:T(8,128)(2,1)S(1)}, u32[]{:S(2)}, u32[]{:S(2)}) collective-permute-start(bf16[64,128]{1,0:T(8,128)(2,1)S(1)} %get-tuple-element.10.refs_8_), channel_id=1, source_target_pairs={{0,128},{1,161},{2,194},{3,227},{4,196},{5,229},{6,134},{7,167},{3... | collective-permute-start | bytes 49160 | tf_op jit(solution)/shard_map/ppermute | solution.py:272
  6.8 0.7 %collective-permute-start.3 = (bf16[64,128]{1,0:T(8,128)(2,1)S(1)}, bf16[64,128]{1,0:T(8,128)(2,1)S(1)}, u32[]{:S(2)}, u32[]{:S(2)}) collective-permute-start(bf16[64,128]{1,0:T(8,128)(2,1)S(1)} %get-tuple-element.12.mine), channel_id=1, source_target_pairs={{1,33},{2,66},{3,99},{4,68},{5,101},{7,39},{33,1},{34,98},{35,67},... | collective-permute-start | bytes 49160 | tf_op jit(solution)/shard_map/ppermute | solution.py:278
  7.5 1.3 %collective-permute-start.5 = (bf16[64,128]{1,0:T(8,128)(2,1)S(1)}, bf16[64,128]{1,0:T(8,128)(2,1)S(1)}, u32[]{:S(2)}, u32[]{:S(2)}) collective-permute-start(bf16[64,128]{1,0:T(8,128)(2,1)S(1)} %get-tuple-element.12.mine), channel_id=1, source_target_pairs={{128,256},{129,289},{130,322},{131,355},{132,324},{133,357},{134,2... | collective-permute-start | bytes 49160 | tf_op jit(solution)/shard_map/ppermute | solution.py:277
  8.8 0.0 collective-permute-done.4.prev_1
  8.8 1.3 %collective-permute-start.6 = (bf16[64,128]{1,0:T(8,128)(2,1)S(1)}, bf16[64,128]{1,0:T(8,128)(2,1)S(1)}, u32[]{:S(2)}, u32[]{:S(2)}) collective-permute-start(bf16[64,128]{1,0:T(8,128)(2,1)S(1)} %collective-permute-done.4.prev_1), channel_id=1, source_target_pairs={{128,256},{129,257},{130,258},{131,259},{132,260},{133,261},{134,2... | collective-permute-start | bytes 49160 | tf_op jit(solution)/shard_map/ppermute | solution.py:279
  10.1 0.0 collective-permute-done.3.own
  10.1 7.0 %collective-permute-done.5.prev_2 = bf16[64,128]{1,0:T(8,128)(2,1)S(1)} collective-permute-done((bf16[64,128]{1,0:T(8,128)(2,1)S(1)}, bf16[64,128]{1,0:T(8,128)(2,1)S(1)}, u32[]{:S(2)}, u32[]{:S(2)}) %collective-permute-start.5) | collective-permute-done | bytes 16416 | tf_op jit(solution)/shard_map/ppermute | solution.py:277
  17.1 3.0 %collective-permute-done.6.prev2 = bf16[64,128]{1,0:T(8,128)(2,1)S(1)} collective-permute-done((bf16[64,128]{1,0:T(8,128)(2,1)S(1)}, bf16[64,128]{1,0:T(8,128)(2,1)S(1)}, u32[]{:S(2)}, u32[]{:S(2)}) %collective-permute-start.6) | collective-permute-done | bytes 16416 | tf_op jit(solution)/shard_map/ppermute | solution.py:279
  20.0 0.8 %shard_map.76 = bf16[8,3,64,128]{3,2,1,0:T(8,128)(2,1)} custom-call(bf16[64,128]{1,0:T(8,128)(2,1)S(1)} %get-tuple-element.12.mine, bf16[64,128]{1,0:T(8,128)(2,1)S(1)} %collective-permute-done.3.own, bf16[64,128]{1,0:T(8,128)(2,1)S(1)} %collective-permute-done.4.prev_1, bf16[64,128]{1,0:T(8,128)(2,1)S(1)} %collective-permute-done.5.prev_2, ...), custom_call_target="tpu_custom_call" | custom-call | tf_op jit(solution)/shard_map/pallas_call | solution.py:240
  20.8 0.0 copy-start
  20.8 6.0 %all-to-all-start = ((bf16[8,3,64,128]{3,2,1,0:T(8,128)(2,1)}), bf16[8,3,64,128]{3,2,1,0:T(8,128)(2,1)S(1)}, u32[]{:S(2)}, u32[]{:S(2)}) async-start(bf16[8,3,64,128]{3,2,1,0:T(8,128)(2,1)} %shard_map.76), calls=%async_computation | async-start | bytes 786432 | tf_op jit(solution)/shard_map/all_to_all | solution.py:290
  26.9 1.9 %collective-permute-start.1 = (bf16[144,1024]{1,0:T(8,128)(2,1)S(1)}, bf16[144,1024]{1,0:T(8,128)(2,1)S(1)}, u32[]{:S(2)}, u32[]{:S(2)}) collective-permute-start(bf16[144,1024]{1,0:T(8,128)(2,1)S(1)} %shard_map.75.q0), channel_id=1, source_target_pairs={{0,1},{1,0},{2,3},{3,2},{4,5},{5,4},{6,7},{7,6},{8,9},{9,8},{10,11... | collective-permute-start | bytes 884744 | tf_op jit(solution)/shard_map/ppermute | solution.py:283
  28.8 0.0 collective-permute-done.q1
  28.8 2.4 %collective-permute-start.2 = (bf16[144,1024]{1,0:T(8,128)(2,1)S(1)}, bf16[144,1024]{1,0:T(8,128)(2,1)S(1)}, u32[]{:S(2)}, u32[]{:S(2)}) collective-permute-start(bf16[144,1024]{1,0:T(8,128)(2,1)S(1)} %collective-permute-done.q1), channel_id=1, source_target_pairs={{0,1},{1,0},{2,3},{3,2},{4,5},{5,4},{6,7},{7,6},{8,9},{9,8},{10,11... | collective-permute-start | bytes 884744 | tf_op jit(solution)/shard_map/ppermute | solution.py:284
  31.2 0.0 collective-permute-done.1.q2
  31.2 4.5 %all-to-all-done.k = bf16[8,3,64,128]{3,2,1,0:T(8,128)(2,1)S(1)} async-done(((bf16[8,3,64,128]{3,2,1,0:T(8,128)(2,1)}), bf16[8,3,64,128]{3,2,1,0:T(8,128)(2,1)S(1)}, u32[]{:S(2)}, u32[]{:S(2)}) %all-to-all-start) | async-done | bytes 393248 | tf_op jit(solution)/shard_map/all_to_all | solution.py:290
  35.8 0.0 collective-permute-done.2.q3
  35.8 0.0 copy-done
  35.8 3.3 %shard_map.77 = bf16[4,3,16,512]{3,2,1,0:T(8,128)(2,1)S(1)} custom-call(bf16[144,1024]{1,0:T(8,128)(2,1)S(1)} %shard_map.75.q0, bf16[144,1024]{1,0:T(8,128)(2,1)S(1)} %collective-permute-done.q1, bf16[144,1024]{1,0:T(8,128)(2,1)S(1)} %collective-permute-done.1.q2, bf16[144,1024]{1,0:T(8,128)(2,1)S(1)} %collective-permute-done.2.q3, ...), custom_call_target="tpu_custom_call" | custom-call | tf_op jit(solution)/shard_map/pallas_call | solution.py:240
  39.0 9.0 %all_to_all.10.parts = bf16[4,3,16,512]{3,2,1,0:T(8,128)(2,1)S(1)} all-to-all(bf16[4,3,16,512]{3,2,1,0:T(8,128)(2,1)S(1)} %shard_map.77), channel_id=1, replica_groups=mesh['zh'=4,'zl'=4,'x'=4,'yh'=2,'yl'=2,'core'=2] {'yl','core'}, dimensions={0} | all-to-all | bytes 393216 | tf_op jit(solution)/shard_map/all_to_all | solution.py:298
  48.0 0.9 %shard_map.78 = f32[16,8192]{1,0:T(8,128)} custom-call(bf16[4,3,16,512]{3,2,1,0:T(8,128)(2,1)S(1)} %all_to_all.10.parts), custom_call_target="tpu_custom_call" | custom-call | tf_op jit(solution)/shard_map/pallas_call | solution.py:240
Async XLA Ops:
  2.6 26.2 %collective-permute-start = (bf16[144,1024]{1,0:T(8,128)(2,1)S(1)}, bf16[144,1024]{1,0:T(8,128)(2,1)S(1)}, u32[]{:S(2)}, u32[]{:S(2)}) collective-permute-start(bf16[144,1024]{1,0:T(8,128)(2,1)S(1)} %shard_map.75.q0), channel_id=1, source_target_pairs={{0,2},{2,0},{1,3},{3,1},{4,6},{6,4},{5,7},{7,5},{8,10},{10,8},{9,1... | collective-permute-start | bytes 884744 | tf_op jit(solution)/shard_map/ppermute | solution.py:282
  6.1 2.6 %collective-permute-start.4 = (bf16[64,128]{1,0:T(8,128)(2,1)S(1)}, bf16[64,128]{1,0:T(8,128)(2,1)S(1)}, u32[]{:S(2)}, u32[]{:S(2)}) collective-permute-start(bf16[64,128]{1,0:T(8,128)(2,1)S(1)} %get-tuple-element.10.refs_8_), channel_id=1, source_target_pairs={{0,128},{1,161},{2,194},{3,227},{4,196},{5,229},{6,134},{7,167},{3... | collective-permute-start | bytes 49160 | tf_op jit(solution)/shard_map/ppermute | solution.py:272
  6.8 3.3 %collective-permute-start.3 = (bf16[64,128]{1,0:T(8,128)(2,1)S(1)}, bf16[64,128]{1,0:T(8,128)(2,1)S(1)}, u32[]{:S(2)}, u32[]{:S(2)}) collective-permute-start(bf16[64,128]{1,0:T(8,128)(2,1)S(1)} %get-tuple-element.12.mine), channel_id=1, source_target_pairs={{1,33},{2,66},{3,99},{4,68},{5,101},{7,39},{33,1},{34,98},{35,67},... | collective-permute-start | bytes 49160 | tf_op jit(solution)/shard_map/ppermute | solution.py:278
  7.5 9.6 %collective-permute-start.5 = (bf16[64,128]{1,0:T(8,128)(2,1)S(1)}, bf16[64,128]{1,0:T(8,128)(2,1)S(1)}, u32[]{:S(2)}, u32[]{:S(2)}) collective-permute-start(bf16[64,128]{1,0:T(8,128)(2,1)S(1)} %get-tuple-element.12.mine), channel_id=1, source_target_pairs={{128,256},{129,289},{130,322},{131,355},{132,324},{133,357},{134,2... | collective-permute-start | bytes 49160 | tf_op jit(solution)/shard_map/ppermute | solution.py:277
  8.8 11.2 %collective-permute-start.6 = (bf16[64,128]{1,0:T(8,128)(2,1)S(1)}, bf16[64,128]{1,0:T(8,128)(2,1)S(1)}, u32[]{:S(2)}, u32[]{:S(2)}) collective-permute-start(bf16[64,128]{1,0:T(8,128)(2,1)S(1)} %collective-permute-done.4.prev_1), channel_id=1, source_target_pairs={{128,256},{129,257},{130,258},{131,259},{132,260},{133,261},{134,2... | collective-permute-start | bytes 49160 | tf_op jit(solution)/shard_map/ppermute | solution.py:279
  20.8 14.9 %copy-start = (s32[64]{0:T(128)S(1)}, s32[64]{0:T(128)}, u32[]{:S(2)}) copy-start(s32[64]{0:T(128)} %param.12) | copy-start | bytes 772
  20.8 14.9 %all-to-all-start = ((bf16[8,3,64,128]{3,2,1,0:T(8,128)(2,1)}), bf16[8,3,64,128]{3,2,1,0:T(8,128)(2,1)S(1)}, u32[]{:S(2)}, u32[]{:S(2)}) async-start(bf16[8,3,64,128]{3,2,1,0:T(8,128)(2,1)} %shard_map.76), calls=%async_computation | async-start | bytes 786432 | tf_op jit(solution)/shard_map/all_to_all | solution.py:290
  26.9 4.3 %collective-permute-start.1 = (bf16[144,1024]{1,0:T(8,128)(2,1)S(1)}, bf16[144,1024]{1,0:T(8,128)(2,1)S(1)}, u32[]{:S(2)}, u32[]{:S(2)}) collective-permute-start(bf16[144,1024]{1,0:T(8,128)(2,1)S(1)} %shard_map.75.q0), channel_id=1, source_target_pairs={{0,1},{1,0},{2,3},{3,2},{4,5},{5,4},{6,7},{7,6},{8,9},{9,8},{10,11... | collective-permute-start | bytes 884744 | tf_op jit(solution)/shard_map/ppermute | solution.py:283
  28.8 7.0 %collective-permute-start.2 = (bf16[144,1024]{1,0:T(8,128)(2,1)S(1)}, bf16[144,1024]{1,0:T(8,128)(2,1)S(1)}, u32[]{:S(2)}, u32[]{:S(2)}) collective-permute-start(bf16[144,1024]{1,0:T(8,128)(2,1)S(1)} %collective-permute-done.q1), channel_id=1, source_target_pairs={{0,1},{1,0},{2,3},{3,2},{4,5},{5,4},{6,7},{7,6},{8,9},{9,8},{10,11... | collective-permute-start | bytes 884744 | tf_op jit(solution)/shard_map/ppermute | solution.py:284
